TPU v7x, 512 devices: a 4x2x32 block of a 4x16x32 slice. The times are simulated.
512 devices in a mesh: groups: 2 (over y), expert: 64 (over z, core), hidden: 4 (over x).
Axes of the slice: x: 4, y: 2, z: 32, core: 2. Of those that a mesh axis runs over, the one named last changes fastest.
The devices are a block of a 4x16x32 slice.
Arguments:
- tokens: bfloat16 [2048, 4096], P(('groups', 'expert')), parts along dimension 0, may hold values from -6 to 6
- expert_ids: int32 [2048, 8], P(('groups', 'expert')), parts along dimension 0, may hold values from 0 to 31, all different within a row; in each aligned block of 16 rows (0 to 15, 16 to 31, ...) at most 8 rows name the same one
- router_scores: float32 [2048, 8], P(('groups', 'expert')), parts along dimension 0, may hold values from 0.05 to 1
- gate_weight: bfloat16 [64, 4096, 512], P('expert', None, 'hidden'), may hold values from -0.09375 to 0.09375
- up_weight: bfloat16 [64, 4096, 512], P('expert', None, 'hidden'), may hold values from -0.09375 to 0.09375
- down_weight: bfloat16 [64, 512, 4096], P('expert', 'hidden'), may hold values from -0.1875 to 0.1875
Outputs:
- moe_out: bfloat16 [2048, 4096], P(('groups', 'expert'), 'hidden'), parts along dimension 0
There are 2 independent parts, one for each index of `groups`. A program takes and returns all parts, laid end to end along the dimension named above; an argument that names none is the same for every part. Nothing has to cross between parts.
Inputs may be any that keep to these rules, and one draw needn't show every extreme that they name: `expert_ids`: each row names 8 different experts. In each aligned block of 16 rows no expert is named by more than 8 rows, a bound that some block reaches.
All inputs are finite; a program needn't handle non-finite values.
Results may differ from a plain program's by a relative error of at most 0.012.
Values may be sent and summed in bfloat16 or wider, within the bound.
No kernel may reach another device: no remote copies, remote signals or barrier semaphores. Data moves between devices by JAX's collectives and lax.ppermute only.
A program may use at most 64 MiB of HBM per device.

v0:
```python
import jax
import jax.numpy as jnp
from jax import lax
from jax.sharding import PartitionSpec as P

SPAN = 2


def body(tokens, expert_ids, router_scores, gate_weight, up_weight, down_weight):
    experts = lax.axis_size("expert") // SPAN
    rows = lax.all_gather(tokens, "expert", axis=0, tiled=True)
    routed = 2.5 * router_scores / jnp.sum(router_scores, axis=1, keepdims=True)
    named = expert_ids[:, :, None] == jnp.arange(experts, dtype=jnp.int32)[None, None, :]
    weight_table = jnp.sum(jnp.where(named, routed[:, :, None], 0.0), axis=1)
    weights_all = lax.all_gather(weight_table, "expert", axis=0, tiled=True)
    mine = lax.axis_index("expert") // SPAN
    weight_col = lax.dynamic_slice_in_dim(weights_all, mine, 1, 1)
    down = lax.all_to_all(down_weight[0], "hidden", split_axis=1, concat_axis=0, tiled=True)
    both = jnp.concatenate([gate_weight[0], up_weight[0]], axis=1)
    width = gate_weight.shape[2]
    val = jnp.dot(rows, both, preferred_element_type=jnp.float32)
    act = (jax.nn.silu(val[:, :width]) * val[:, width:]).astype(jnp.bfloat16)
    act_all = lax.all_gather(act, "hidden", axis=1, tiled=True)
    out = jnp.dot(act_all, down, preferred_element_type=jnp.float32)
    out = (out * weight_col).astype(jnp.bfloat16)
    return lax.psum_scatter(out, "expert", scatter_dimension=0, tiled=True)


def solution(mesh):
    return jax.shard_map(
        body,
        mesh=mesh,
        in_specs=(
            P(("groups", "expert"), None),
            P(("groups", "expert"), None),
            P(("groups", "expert"), None),
            P("expert", None, "hidden"),
            P("expert", None, "hidden"),
            P("expert", "hidden", None),
        ),
        out_specs=P(("groups", "expert"), "hidden"),
        check_vma=False,
    )
```

profile of v0, /device:TPU:34, one launch (start us, length us, event | category | flops | bytes accessed | tf_op | source)
XLA Modules:
  0.0 459.3 jit_solution(4400639572138969000)
XLA Ops:
  6.5 0.0 all-gather.3.cloned.1.call-start
  6.6 0.7 all-gather.3.cloned.1.call-update
  7.3 0.1 all-gather.5.cloned.1.call-start
  7.4 167.8 %all-gather.3.cloned.1.call-done = bf16[1024,4096]{1,0:T(8,128)(2,1)} async-done(((bf16[16,4096]{1,0:T(8,128)(2,1)}), bf16[1024,4096]{1,0:T(8,128)(2,1)}) %all-gather.3.cloned.1.call-update) | async-done | bytes 8388624 | tf_op jit(solution)/shard_map/all_gather | solution.py:11
  175.2 6.5 %fusion.4 = f32[1024,256]{0,1:T(8,128)S(1)} fusion(bf16[1024,4096]{1,0:T(8,128)(2,1)} %all-gather.3.cloned.1.call-done, bf16[4096,128]{1,0:T(8,128)(2,1)} %bitcast.12, bf16[4096,128]{1,0:T(8,128)(2,1)} %bitcast.13), kind=kOutput, calls=%fused_computation.5 | convolution fusion | flops 2151677952 | bytes 11534336 | tf_op jit(solution)/shard_map/dot_general | solution.py:21
  181.7 0.0 copy-start.1
  181.7 0.0 copy-start.2
  181.7 0.9 fusion.7
  182.6 0.1 all-gather.5.cloned.1.call-update
  182.6 0.0 copy-done
  182.7 1.3 copy.19
  184.0 5.2 %all-to-all-start = ((bf16[128,4,1024]{0,2,1:T(8,128)(2,1)}), bf16[128,4,1024]{0,2,1:T(8,128)(2,1)S(1)}, u32[]{:S(2)}, u32[]{:S(2)}) async-start(bf16[128,4,1024]{0,2,1:T(8,128)(2,1)} %bitcast.3), calls=%async_computation | async-start | bytes 2097152 | tf_op jit(solution)/shard_map/all_to_all | solution.py:18
  189.2 0.0 reduce-scatter.2.cloned.1.call-start
  189.2 0.1 copy.22
  189.3 0.1 copy.21
  189.4 0.1 select_reduce_fusion
  189.5 54.6 %all_gather.11 = f32[1024,32]{1,0:T(8,128)S(1)} all-gather(f32[16,32]{1,0:T(8,128)S(1)} %select_reduce_fusion), channel_id=1, replica_groups=mesh['groups'=2,'expert'=64,'hidden'=4] {'expert'}, dimensions={0}, use_global_device_ids=true | all-gather | bytes 133120 | tf_op jit(solution)/shard_map/all_gather | solution.py:15
  244.1 0.4 dynamic-slice_reduce_fusion
  244.5 0.0 all-to-all-done
  244.5 0.5 copy.20
  245.0 0.0 all-gather.5.cloned.1.call-done
  245.0 3.9 multiply_convert_fusion
  248.9 0.1 reduce-scatter.2.cloned.1.call-update
  249.0 203.8 %reduce-scatter.2.cloned.1.call-done = bf16[16,1024]{1,0:T(8,128)(2,1)} async-done(((bf16[1024,1024]{1,0:T(8,128)(2,1)}), bf16[16,1024]{1,0:T(8,128)(2,1)}) %reduce-scatter.2.cloned.1.call-update) | async-done | bytes 32784 | tf_op jit(solution)/shard_map/reduce_scatter | solution.py:26
  (5 shorter events, 0.0 us)
Async XLA Ops:
  6.5 168.7 %all-gather.3.cloned.1.call-start = ((), (), s32[]{:S(2)}) async-start(), calls=%async_computation.2 | async-start | bytes 8519680 | tf_op jit(solution)/shard_map/all_gather | solution.py:11
  7.3 237.7 %all-gather.5.cloned.1.call-start = ((), (), s32[]{:S(2)}) async-start(), calls=%async_computation.3 | async-start | bytes 1310720 | tf_op jit(solution)/shard_map/all_gather | solution.py:23
  175.2 7.4 %copy-start = (bf16[1,128,4096]{2,1,0:T(8,128)(2,1)S(1)}, bf16[1,128,4096]{2,1,0:T(8,128)(2,1)}, u32[]{:S(2)}) copy-start(bf16[1,128,4096]{2,1,0:T(8,128)(2,1)} %param.11) | copy-start | bytes 3145732
  181.7 7.5 %copy-start.1 = (f32[16,8]{0,1:T(8,128)S(1)}, f32[16,8]{0,1:T(8,128)}, u32[]{:S(2)}) copy-start(f32[16,8]{0,1:T(8,128)} %param.8) | copy-start | bytes 1540
  181.7 7.6 %copy-start.2 = (s32[16,8]{0,1:T(8,128)S(1)}, s32[16,8]{0,1:T(8,128)}, u32[]{:S(2)}) copy-start(s32[16,8]{0,1:T(8,128)} %param.7) | copy-start | bytes 1540
  184.0 60.5 %all-to-all-start = ((bf16[128,4,1024]{0,2,1:T(8,128)(2,1)}), bf16[128,4,1024]{0,2,1:T(8,128)(2,1)S(1)}, u32[]{:S(2)}, u32[]{:S(2)}) async-start(bf16[128,4,1024]{0,2,1:T(8,128)(2,1)} %bitcast.3), calls=%async_computation | async-start | bytes 2097152 | tf_op jit(solution)/shard_map/all_to_all | solution.py:18
  189.2 263.6 %reduce-scatter.2.cloned.1.call-start = ((), (), s32[]{:S(2)}) async-start(), calls=%async_computation.4 | async-start | bytes 2129920 | tf_op jit(solution)/shard_map/reduce_scatter | solution.py:26
Sparse Core Ops, SparseCore 0:
  9.5 165.6 all-gather.2
  182.8 30.5 all-gather.4
  249.1 203.5 reduce-scatter.1
where the time goes:
time: 459 us
  waiting for transfers between devices  372 us (81%)
  blocking collectives  54.6 us (12%)
  between operations  13.2 us (3%)
  matrix products  10.3 us (2%)
  starting transfers between devices  5.27 us (1%)
    reduce_scatter x1, waiting for transfers between devices, body(): return lax.psum_scatter(out, 'expert', scatter_dimension=0, tiled=True)  204 us
    all_gather x1, waiting for transfers between devices, body(): rows = lax.all_gather(tokens, 'expert', axis=0, tiled=True)  168 us
    all_gather x1, blocking collectives, body(): weights_all = lax.all_gather(weight_table, 'expert', axis=0, tiled=True)  54.6 us
  transfers between devices with their start and end apart: 4, of which 2 were waited for; matrix products, arithmetic and copies ran while one was open for 1% of the time, Pallas kernels for 0%

commit v1 on v0

--- a/solution.py
+++ b/solution.py
@@ -12,7 +12,10 @@
     routed = 2.5 * router_scores / jnp.sum(router_scores, axis=1, keepdims=True)
     named = expert_ids[:, :, None] == jnp.arange(experts, dtype=jnp.int32)[None, None, :]
     weight_table = jnp.sum(jnp.where(named, routed[:, :, None], 0.0), axis=1)
-    weights_all = lax.all_gather(weight_table, "expert", axis=0, tiled=True)
+    size = lax.axis_size("expert")
+    tiles = jnp.stack([weight_table for _ in range(size)])
+    tiles = lax.all_to_all(tiles, "expert", split_axis=0, concat_axis=0)
+    weights_all = jnp.concatenate(tiles, axis=0)
     mine = lax.axis_index("expert") // SPAN
     weight_col = lax.dynamic_slice_in_dim(weights_all, mine, 1, 1)
     down = lax.all_to_all(down_weight[0], "hidden", split_axis=1, concat_axis=0, tiled=True)

time: 459 us -> 438 us (0.954)
  blocking collectives: 54.6 us -> 0 us
  starting transfers between devices: 5.27 us -> 58.6 us
  waiting for transfers between devices: 372 us -> 349 us
    all_gather x1 -> x0, blocking collectives: 54.6 us -> none  [body(): weights_all = lax.all_gather(weight_table, 'expert', axis=0, tiled=True)]
    all_gather x1, waiting for transfers between devices: 168 us -> 122 us  [body(): rows = lax.all_gather(tokens, 'expert', axis=0, tiled=True)]
    all_to_all x1, starting transfers between devices: 5.2 us -> 43.9 us  [body(): lax.all_to_all(down_weight[0], 'hidden', split_axis=1, concat_axis=0, til...]
    all_to_all x0 -> x1, waiting for transfers between devices: none -> 29.8 us  [body(): tiles = lax.all_to_all(tiles, 'expert', split_axis=0, concat_axis=0)]
    all_to_all x0 -> x1, starting transfers between devices: none -> 14.6 us  [body(): tiles = lax.all_to_all(tiles, 'expert', split_axis=0, concat_axis=0)]
    reduce_scatter x1, waiting for transfers between devices: 204 us -> 196 us  [body(): return lax.psum_scatter(out, 'expert', scatter_dimension=0, tiled=True)]
  transfers between devices with their start and end apart: 4 -> 5, of which waited for: 2 -> 3; matrix products, arithmetic and copies ran while one was open for 1% -> 3% of each run, Pallas kernels for 0% -> 0%
where the time goes in v1:
time: 438 us; the launch traced here: 437 us
  waiting for transfers between devices  349 us (80%)
  starting transfers between devices  58.6 us (13%)
  between operations  13.2 us (3%)
  matrix products  9.73 us (2%)
  local copies, waits for them, and re-layouts  5.02 us (1%)
    reduce_scatter x1, waiting for transfers between devices, body(): return lax.psum_scatter(out, 'expert', scatter_dimension=0, tiled=True)  196 us
    all_gather x1, waiting for transfers between devices, body(): rows = lax.all_gather(tokens, 'expert', axis=0, tiled=True)  122 us
    all_to_all x1, starting transfers between devices, body(): lax.all_to_all(down_weight[0], 'hidden', split_axis=1, concat_axis=0, til...  43.9 us
    all_to_all x1, waiting for transfers between devices, body(): tiles = lax.all_to_all(tiles, 'expert', split_axis=0, concat_axis=0)  29.8 us
    all_to_all x1, starting transfers between devices, body(): tiles = lax.all_to_all(tiles, 'expert', split_axis=0, concat_axis=0)  14.6 us
  transfers between devices with their start and end apart: 5, of which 3 were waited for; matrix products, arithmetic and copies ran while one was open for 3% of the time, Pallas kernels for 0%

profile of v1, /device:TPU:34, one launch (start us, length us, event | category | flops | bytes accessed | tf_op | source)
XLA Modules:
  0.0 437.3 jit_solution(12405510523816569268)
XLA Ops:
  6.6 0.7 all-gather.3.cloned.1.call-update
  7.3 2.3 copy.15
  9.6 43.9 %all-to-all-start = ((bf16[128,4,1024]{0,2,1:T(8,128)(2,1)}), bf16[128,4,1024]{0,2,1:T(8,128)(2,1)S(1)}, u32[]{:S(2)}, u32[]{:S(2)}) async-start(bf16[128,4,1024]{0,2,1:T(8,128)(2,1)} %bitcast.3), calls=%async_computation | async-start | bytes 2097152 | tf_op jit(solution)/shard_map/all_to_all | solution.py:21
  53.5 121.7 %all-gather.3.cloned.1.call-done = bf16[1024,4096]{1,0:T(8,128)(2,1)} async-done(((bf16[16,4096]{1,0:T(8,128)(2,1)}), bf16[1024,4096]{1,0:T(8,128)(2,1)}) %all-gather.3.cloned.1.call-update) | async-done | bytes 8388624 | tf_op jit(solution)/shard_map/all_gather | solution.py:11
  175.2 5.9 %fusion.4 = f32[1024,256]{0,1:T(8,128)S(1)} fusion(bf16[1024,4096]{1,0:T(8,128)(2,1)} %all-gather.3.cloned.1.call-done, bf16[4096,128]{1,0:T(8,128)(2,1)S(1)} %bitcast.14, bf16[4096,128]{1,0:T(8,128)(2,1)S(1)} %bitcast.15), kind=kOutput, calls=%fused_computation.5 | convolution fusion | flops 2151677952 | bytes 11534336 | tf_op jit(solution)/shard_map/dot_general | solution.py:24
  181.1 0.8 fusion.7
  182.0 0.1 all-gather.5.cloned.1.call-update
  182.1 0.1 copy.18
  182.1 0.1 copy.17
  182.2 0.1 select_reduce_fusion
  182.4 0.9 reshape.14
  183.3 0.0 all-to-all-done
  183.3 14.6 %all-to-all-start.1 = ((f32[64,1,512]{2,1,0:T(1,128)}), f32[64,1,512]{2,1,0:T(1,128)S(1)}, u32[]{:S(2)}, u32[]{:S(2)}) async-start(f32[64,1,512]{2,1,0:T(1,128)} %reshape.14), calls=%async_computation.1 | async-start | bytes 262144 | tf_op jit(solution)/shard_map/all_to_all | solution.py:17
  198.0 0.1 reduce-scatter.2.cloned.1.call-start
  198.0 0.5 copy.16
  198.6 29.8 %all-to-all-done.1 = f32[64,1,512]{2,1,0:T(1,128)S(1)} async-done(((f32[64,1,512]{2,1,0:T(1,128)}), f32[64,1,512]{2,1,0:T(1,128)S(1)}, u32[]{:S(2)}, u32[]{:S(2)}) %all-to-all-start.1) | async-done | bytes 131104 | tf_op jit(solution)/shard_map/all_to_all | solution.py:17
  228.4 0.5 broadcast.9
  228.9 0.9 reduce.2
  229.9 0.2 reshape.15
  230.0 0.4 dynamic-slice_reduce_fusion
  230.4 0.0 all-gather.5.cloned.1.call-done
  230.4 3.9 multiply_convert_fusion
  234.3 0.1 reduce-scatter.2.cloned.1.call-update
  234.4 196.4 %reduce-scatter.2.cloned.1.call-done = bf16[16,1024]{1,0:T(8,128)(2,1)} async-done(((bf16[1024,1024]{1,0:T(8,128)(2,1)}), bf16[16,1024]{1,0:T(8,128)(2,1)}) %reduce-scatter.2.cloned.1.call-update) | async-done | bytes 32784 | tf_op jit(solution)/shard_map/reduce_scatter | solution.py:29
  (13 shorter events, 0.1 us)
Async XLA Ops:
  6.5 168.7 %copy-start.2 = (bf16[1,4096,128]{2,1,0:T(8,128)(2,1)S(1)}, bf16[1,4096,128]{2,1,0:T(8,128)(2,1)}, u32[]{:S(2)}) copy-start(bf16[1,4096,128]{2,1,0:T(8,128)(2,1)} %param.10) | copy-start | bytes 3145732
  6.5 168.7 %copy-start.3 = (bf16[1,4096,128]{2,1,0:T(8,128)(2,1)S(1)}, bf16[1,4096,128]{2,1,0:T(8,128)(2,1)}, u32[]{:S(2)}) copy-start(bf16[1,4096,128]{2,1,0:T(8,128)(2,1)} %param.9) | copy-start | bytes 3145732
  6.6 168.7 %all-gather.3.cloned.1.call-start = ((), (), s32[]{:S(2)}) async-start(), calls=%async_computation.3 | async-start | bytes 8519680 | tf_op jit(solution)/shard_map/all_gather | solution.py:11
  9.6 173.7 %all-to-all-start = ((bf16[128,4,1024]{0,2,1:T(8,128)(2,1)}), bf16[128,4,1024]{0,2,1:T(8,128)(2,1)S(1)}, u32[]{:S(2)}, u32[]{:S(2)}) async-start(bf16[128,4,1024]{0,2,1:T(8,128)(2,1)} %bitcast.3), calls=%async_computation | async-start | bytes 2097152 | tf_op jit(solution)/shard_map/all_to_all | solution.py:21
  53.5 176.9 %all-gather.5.cloned.1.call-start = ((), (), s32[]{:S(2)}) async-start(), calls=%async_computation.4 | async-start | bytes 1310720 | tf_op jit(solution)/shard_map/all_gather | solution.py:26
  175.2 6.8 %copy-start = (f32[16,8]{0,1:T(8,128)S(1)}, f32[16,8]{0,1:T(8,128)}, u32[]{:S(2)}) copy-start(f32[16,8]{0,1:T(8,128)} %param.8) | copy-start | bytes 1540
  175.2 6.9 %copy-start.1 = (s32[16,8]{0,1:T(8,128)S(1)}, s32[16,8]{0,1:T(8,128)}, u32[]{:S(2)}) copy-start(s32[16,8]{0,1:T(8,128)} %param.7) | copy-start | bytes 1540
  183.3 45.1 %all-to-all-start.1 = ((f32[64,1,512]{2,1,0:T(1,128)}), f32[64,1,512]{2,1,0:T(1,128)S(1)}, u32[]{:S(2)}, u32[]{:S(2)}) async-start(f32[64,1,512]{2,1,0:T(1,128)} %reshape.14), calls=%async_computation.1 | async-start | bytes 262144 | tf_op jit(solution)/shard_map/all_to_all | solution.py:17
  198.0 232.8 %reduce-scatter.2.cloned.1.call-start = ((), (), s32[]{:S(2)}) async-start(), calls=%async_computation.5 | async-start | bytes 2129920 | tf_op jit(solution)/shard_map/reduce_scatter | solution.py:29
Sparse Core Ops, SparseCore 0:
  9.5 165.6 all-gather.2
  182.1 30.8 all-gather.4
  234.5 196.2 reduce-scatter.1
